TPU v7x, 32 devices: a whole 2x2x4 slice. The times are simulated.
32 devices in a mesh: level: 2 (over core), gx: 4 (over y, x), yz: 4 (over z).
Axes of the slice: x: 2, y: 2, z: 4, core: 2. Of those that a mesh axis runs over, the one named last changes fastest.
Arguments:
- init_field: float32 [128, 64, 256], P('gx', 'yz'), may hold values from -6 to 6
- source: float32 [128, 64, 256], P('gx', 'yz'), may hold values from -4 to 4
- damping: float32 [128, 64, 256], P('gx', 'yz'), may hold values from 0.05 to 2
Outputs:
- final_states: float32 [2, 128, 64, 256], P('level', 'gx', 'yz')
All inputs are finite; a program needn't handle non-finite values.
Results may differ from a plain program's by a relative error of at most 0.0001.
Values sent between devices are 32-bit elements; how exact they have to be, the bound alone decides.
A program may use at most 64 MiB of HBM per device.

v0:
```python
import jax
import jax.numpy as jnp
from jax import lax
from jax.sharding import PartitionSpec as P

STEPS = 3
ITERS = 3
diffusion_number = 1.0


def extended(cells, sides, width):
    for axis, dim in sides:
        count = lax.axis_size(axis)
        ends = count - 1
        head = lax.slice_in_dim(cells, 0, width, axis=dim)
        tail = lax.slice_in_dim(cells, cells.shape[dim] - width, cells.shape[dim], axis=dim)
        cells = jnp.concatenate(
            [
                lax.ppermute(tail, axis, [(i, (i + 1) % count) for i in range(ends)]),
                cells,
                lax.ppermute(head, axis, [((i + 1) % count, i) for i in range(ends)]),
            ],
            axis=dim,
        )
    return cells


def passed_along(block, axis, distance):
    devices = range(lax.axis_size(axis))
    route = [(i - distance, i) for i in devices if i - distance in devices]
    return lax.ppermute(block, axis, route)


def stencil_from(padded, field, damping):
    beside = padded[2:, 1:-1, :] + padded[:-2, 1:-1, :]
    beside = beside + padded[1:-1, 2:, :] + padded[1:-1, :-2, :]
    zero_plane = jnp.zeros_like(field[:, :, :1])
    beside = beside + jnp.concatenate([field[:, :, 1:], zero_plane], axis=2)
    beside = beside + jnp.concatenate([zero_plane, field[:, :, :-1]], axis=2)
    return damping * field + diffusion_number * (6.0 * field - beside)


def operate(field, damping):
    padded = extended(field, (("gx", 0), ("yz", 1)), 1)
    return field + stencil_from(padded, field, damping)


def two_products(resid, image):
    return lax.psum((jnp.sum(resid * resid), jnp.sum(resid * image)), ("gx", "yz"))


def solve(target, guess, damping):
    answer = guess
    resid = target - operate(answer, damping)
    image = operate(resid, damping)
    norm_now, product = two_products(resid, image)
    alpha = norm_now / product
    direction, along = (resid, image)
    for step in range(ITERS):
        answer = answer + alpha * direction
        resid = resid - alpha * along
        if step + 1 < ITERS:
            image = operate(resid, damping)
            norm_next, product = two_products(resid, image)
            ratio = norm_next / norm_now
            alpha = norm_next / (product - ratio * norm_next / alpha)
            direction = resid + ratio * direction
            along = image + ratio * along
            norm_now = norm_next
    return answer


def per_device(init_field, source, damping):
    upper = lax.axis_index("level") == 1
    state = init_field
    older = jnp.where(upper, init_field, jnp.zeros_like(init_field))
    for rounds in range(STEPS + 1):
        if rounds == 0:
            extra = jnp.zeros_like(init_field)
        else:
            incoming = passed_along(state, "level", 1)
            change = incoming - older
            older = incoming
            padded = extended(change, (("gx", 0), ("yz", 1)), 1)
            extra = 0.5 * stencil_from(padded, change, damping)
        fresh = solve(state + source + extra, state, damping)
        if rounds == 0:
            state = jnp.where(upper, state, fresh)
        elif rounds == STEPS:
            state = jnp.where(upper, fresh, state)
        else:
            state = fresh
    return state[None]


def solution(mesh):
    in_specs = (P("gx", "yz", None), P("gx", "yz", None), P("gx", "yz", None))
    out_specs = P("level", "gx", "yz", None)
    return jax.shard_map(
        per_device, mesh=mesh, in_specs=in_specs, out_specs=out_specs, check_vma=False
    )
```

profile of v0, /device:TPU:0, one launch (start us, length us, event | category | flops | bytes accessed | tf_op | source)
XLA Modules:
  0.0 858.0 jit_solution(10552199963659555347)
XLA Ops:
  38.3 40.1 %all-reduce.49 = (f32[]{:T(128)}, f32[]{:T(128)}) all-reduce(f32[]{:T(128)} %get-tuple-element.28, f32[]{:T(128)} %get-tuple-element.27), channel_id=1, replica_groups=mesh['level'=2,'gx'=4,'yz'=4] {'gx','yz'}, use_global_device_ids=true, to_apply=%region_1.2 | all-reduce | flops 2 | bytes 16 | tf_op jit(solution)/shard_map/psum | solution.py:49
  83.3 8.2 collective-permute-done.8
  100.9 39.7 %all-reduce.48 = (f32[]{:T(128)}, f32[]{:T(128)}) all-reduce(f32[]{:T(128)} %get-tuple-element.26, f32[]{:T(128)} %get-tuple-element.25), channel_id=1, replica_groups=mesh['level'=2,'gx'=4,'yz'=4] {'gx','yz'}, use_global_device_ids=true, to_apply=%region_5.6 | all-reduce | flops 2 | bytes 16 | tf_op jit(solution)/shard_map/psum | solution.py:49
  149.0 5.5 collective-permute-done.12
  163.2 39.7 %all-reduce.47 = (f32[]{:T(128)}, f32[]{:T(128)}) all-reduce(f32[]{:T(128)} %get-tuple-element.24, f32[]{:T(128)} %get-tuple-element.23), channel_id=1, replica_groups=mesh['level'=2,'gx'=4,'yz'=4] {'gx','yz'}, use_global_device_ids=true, to_apply=%region_9.10 | all-reduce | flops 2 | bytes 16 | tf_op jit(solution)/shard_map/psum | solution.py:49
  212.1 7.1 collective-permute-start.18
  255.8 39.8 %all-reduce.46 = (f32[]{:T(128)}, f32[]{:T(128)}) all-reduce(f32[]{:T(128)} %get-tuple-element.22, f32[]{:T(128)} %get-tuple-element.21), channel_id=1, replica_groups=mesh['level'=2,'gx'=4,'yz'=4] {'gx','yz'}, use_global_device_ids=true, to_apply=%region_13.14 | all-reduce | flops 2 | bytes 16 | tf_op jit(solution)/shard_map/psum | solution.py:49
  299.6 8.9 %collective-permute-done.29 = f32[1,16,256]{2,1,0:T(8,128)S(1)} collective-permute-done((f32[1,16,256]{2,1,0:T(8,128)S(1)}, f32[1,16,256]{2,1,0:T(8,128)S(1)}, u32[]{:S(2)}, u32[]{:S(2)}) %collective-permute-start.29) | collective-permute-done | bytes 16416 | tf_op jit(solution)/shard_map/ppermute | solution.py:21
  317.9 39.7 %all-reduce.45 = (f32[]{:T(128)}, f32[]{:T(128)}) all-reduce(f32[]{:T(128)} %get-tuple-element.20, f32[]{:T(128)} %get-tuple-element.19), channel_id=1, replica_groups=mesh['level'=2,'gx'=4,'yz'=4] {'gx','yz'}, use_global_device_ids=true, to_apply=%region_17.18 | all-reduce | flops 2 | bytes 16 | tf_op jit(solution)/shard_map/psum | solution.py:49
  366.0 5.5 collective-permute-done.33
  380.0 39.7 %all-reduce.44 = (f32[]{:T(128)}, f32[]{:T(128)}) all-reduce(f32[]{:T(128)} %get-tuple-element.18, f32[]{:T(128)} %get-tuple-element.17), channel_id=1, replica_groups=mesh['level'=2,'gx'=4,'yz'=4] {'gx','yz'}, use_global_device_ids=true, to_apply=%region_21.22 | all-reduce | flops 2 | bytes 16 | tf_op jit(solution)/shard_map/psum | solution.py:49
  428.8 7.2 collective-permute-start.39
  451.7 5.4 collective-permute-start.47
  472.6 39.8 %all-reduce.43 = (f32[]{:T(128)}, f32[]{:T(128)}) all-reduce(f32[]{:T(128)} %get-tuple-element.16, f32[]{:T(128)} %get-tuple-element.15), channel_id=1, replica_groups=mesh['level'=2,'gx'=4,'yz'=4] {'gx','yz'}, use_global_device_ids=true, to_apply=%region_25.26 | all-reduce | flops 2 | bytes 16 | tf_op jit(solution)/shard_map/psum | solution.py:49
  516.4 8.9 %collective-permute-done.50 = f32[1,16,256]{2,1,0:T(8,128)S(1)} collective-permute-done((f32[1,16,256]{2,1,0:T(8,128)S(1)}, f32[1,16,256]{2,1,0:T(8,128)S(1)}, u32[]{:S(2)}, u32[]{:S(2)}) %collective-permute-start.50) | collective-permute-done | bytes 16416 | tf_op jit(solution)/shard_map/ppermute | solution.py:21
  534.7 39.8 %all-reduce.42 = (f32[]{:T(128)}, f32[]{:T(128)}) all-reduce(f32[]{:T(128)} %get-tuple-element.14, f32[]{:T(128)} %get-tuple-element.13), channel_id=1, replica_groups=mesh['level'=2,'gx'=4,'yz'=4] {'gx','yz'}, use_global_device_ids=true, to_apply=%region_29.30 | all-reduce | flops 2 | bytes 16 | tf_op jit(solution)/shard_map/psum | solution.py:49
  596.9 39.7 %all-reduce.41 = (f32[]{:T(128)}, f32[]{:T(128)}) all-reduce(f32[]{:T(128)} %get-tuple-element.12, f32[]{:T(128)} %get-tuple-element.11), channel_id=1, replica_groups=mesh['level'=2,'gx'=4,'yz'=4] {'gx','yz'}, use_global_device_ids=true, to_apply=%region_33.34 | all-reduce | flops 2 | bytes 16 | tf_op jit(solution)/shard_map/psum | solution.py:49
  644.9 7.2 collective-permute-start.60
  667.8 5.4 collective-permute-start.68
  688.6 39.8 %all-reduce.40 = (f32[]{:T(128)}, f32[]{:T(128)}) all-reduce(f32[]{:T(128)} %get-tuple-element.10, f32[]{:T(128)} %get-tuple-element.9), channel_id=1, replica_groups=mesh['level'=2,'gx'=4,'yz'=4] {'gx','yz'}, use_global_device_ids=true, to_apply=%region_37.38 | all-reduce | flops 2 | bytes 16 | tf_op jit(solution)/shard_map/psum | solution.py:49
  732.7 8.9 %collective-permute-done.71 = f32[1,16,256]{2,1,0:T(8,128)S(1)} collective-permute-done((f32[1,16,256]{2,1,0:T(8,128)S(1)}, f32[1,16,256]{2,1,0:T(8,128)S(1)}, u32[]{:S(2)}, u32[]{:S(2)}) %collective-permute-start.71) | collective-permute-done | bytes 16416 | tf_op jit(solution)/shard_map/ppermute | solution.py:21
  751.0 39.7 %all-reduce.39 = (f32[]{:T(128)}, f32[]{:T(128)}) all-reduce(f32[]{:T(128)} %get-tuple-element.8, f32[]{:T(128)} %get-tuple-element.7), channel_id=1, replica_groups=mesh['level'=2,'gx'=4,'yz'=4] {'gx','yz'}, use_global_device_ids=true, to_apply=%region_41.42 | all-reduce | flops 2 | bytes 16 | tf_op jit(solution)/shard_map/psum | solution.py:49
  799.2 5.5 collective-permute-done.75
  813.3 39.7 %all-reduce.38 = (f32[]{:T(128)}, f32[]{:T(128)}) all-reduce(f32[]{:T(128)} %get-tuple-element.6, f32[]{:T(128)} %get-tuple-element.5), channel_id=1, replica_groups=mesh['level'=2,'gx'=4,'yz'=4] {'gx','yz'}, use_global_device_ids=true, to_apply=%region_45.46 | all-reduce | flops 2 | bytes 16 | tf_op jit(solution)/shard_map/psum | solution.py:49
  (257 shorter events, 257.5 us)
Async XLA Ops:
  81.9 9.6 %collective-permute-start.8 = (f32[1,16,256]{2,1,0:T(8,128)S(1)}, f32[1,16,256]{2,1,0:T(8,128)S(1)}, u32[]{:S(2)}, u32[]{:S(2)}) collective-permute-start(f32[1,16,256]{2,1,0:T(8,128)S(1)} %get-tuple-element.164), channel_id=1, source_target_pairs={{4,0},{8,4},{12,8},{5,1},{9,5},{13,9},{6,2},{10,6},{14,10},{7,3},{... | collective-permute-start | bytes 49160 | tf_op jit(solution)/shard_map/ppermute | solution.py:21
  147.6 7.0 collective-permute-start.12
  208.4 12.0 %collective-permute-start.22 = (f32[1,16,256]{2,1,0:T(8,128)S(1)}, f32[1,16,256]{2,1,0:T(8,128)S(1)}, u32[]{:S(2)}, u32[]{:S(2)}) collective-permute-start(f32[1,16,256]{2,1,0:T(8,128)S(1)} %get-tuple-element.157), channel_id=1, source_target_pairs={{0,4},{4,8},{8,12},{1,5},{5,9},{9,13},{2,6},{6,10},{10,14},{3,7},{... | collective-permute-start | bytes 49160 | tf_op jit(solution)/shard_map/ppermute | solution.py:19
  209.7 10.7 %collective-permute-start.21 = (f32[1,16,256]{2,1,0:T(8,128)S(1)}, f32[1,16,256]{2,1,0:T(8,128)S(1)}, u32[]{:S(2)}, u32[]{:S(2)}) collective-permute-start(f32[1,16,256]{2,1,0:T(8,128)S(1)} %get-tuple-element.158), channel_id=1, source_target_pairs={{4,0},{8,4},{12,8},{5,1},{9,5},{13,9},{6,2},{10,6},{14,10},{7,3},{... | collective-permute-start | bytes 49160 | tf_op jit(solution)/shard_map/ppermute | solution.py:21
  212.1 14.3 %collective-permute-start.18 = (f32[1,16,256]{2,1,0:T(8,128)S(1)}, f32[1,16,256]{2,1,0:T(8,128)S(1)}, u32[]{:S(2)}, u32[]{:S(2)}) collective-permute-start(f32[1,16,256]{2,1,0:T(8,128)S(1)} %get-tuple-element.155), channel_id=1, source_target_pairs={{0,4},{4,8},{8,12},{1,5},{5,9},{9,13},{2,6},{6,10},{10,14},{3,7},{... | collective-permute-start | bytes 49160 | tf_op jit(solution)/shard_map/ppermute | solution.py:19
  219.2 7.2 collective-permute-start.17
  220.5 12.2 %collective-permute-start.23 = (f32[34,1,256]{2,1,0:T(1,128)S(1)}, f32[34,1,256]{2,1,0:T(1,128)S(1)}, u32[]{:S(2)}, u32[]{:S(2)}) collective-permute-start(f32[34,1,256]{2,1,0:T(1,128)S(1)} %get-tuple-element.89), channel_id=1, source_target_pairs={{1,0},{2,1},{3,2},{5,4},{6,5},{7,6},{9,8},{10,9},{11,10},{13,12},{... | collective-permute-start | bytes 104456 | tf_op jit(solution)/shard_map/ppermute | solution.py:21
  221.8 10.9 %collective-permute-start.24 = (f32[34,1,256]{2,1,0:T(1,128)S(1)}, f32[34,1,256]{2,1,0:T(1,128)S(1)}, u32[]{:S(2)}, u32[]{:S(2)}) collective-permute-start(f32[34,1,256]{2,1,0:T(1,128)S(1)} %get-tuple-element.90), channel_id=1, source_target_pairs={{0,1},{1,2},{2,3},{4,5},{5,6},{6,7},{8,9},{9,10},{10,11},{12,13},{... | collective-permute-start | bytes 104456 | tf_op jit(solution)/shard_map/ppermute | solution.py:19
  298.2 10.3 %collective-permute-start.29 = (f32[1,16,256]{2,1,0:T(8,128)S(1)}, f32[1,16,256]{2,1,0:T(8,128)S(1)}, u32[]{:S(2)}, u32[]{:S(2)}) collective-permute-start(f32[1,16,256]{2,1,0:T(8,128)S(1)} %get-tuple-element.144), channel_id=1, source_target_pairs={{4,0},{8,4},{12,8},{5,1},{9,5},{13,9},{6,2},{10,6},{14,10},{7,3},{... | collective-permute-start | bytes 49160 | tf_op jit(solution)/shard_map/ppermute | solution.py:21
  425.0 12.3 %collective-permute-start.43 = (f32[1,16,256]{2,1,0:T(8,128)S(1)}, f32[1,16,256]{2,1,0:T(8,128)S(1)}, u32[]{:S(2)}, u32[]{:S(2)}) collective-permute-start(f32[1,16,256]{2,1,0:T(8,128)S(1)} %get-tuple-element.137), channel_id=1, source_target_pairs={{0,4},{4,8},{8,12},{1,5},{5,9},{9,13},{2,6},{6,10},{10,14},{3,7},{... | collective-permute-start | bytes 49160 | tf_op jit(solution)/shard_map/ppermute | solution.py:19
  426.3 11.0 %collective-permute-start.42 = (f32[1,16,256]{2,1,0:T(8,128)S(1)}, f32[1,16,256]{2,1,0:T(8,128)S(1)}, u32[]{:S(2)}, u32[]{:S(2)}) collective-permute-start(f32[1,16,256]{2,1,0:T(8,128)S(1)} %get-tuple-element.138), channel_id=1, source_target_pairs={{4,0},{8,4},{12,8},{5,1},{9,5},{13,9},{6,2},{10,6},{14,10},{7,3},{... | collective-permute-start | bytes 49160 | tf_op jit(solution)/shard_map/ppermute | solution.py:21
  428.8 14.4 %collective-permute-start.39 = (f32[1,16,256]{2,1,0:T(8,128)S(1)}, f32[1,16,256]{2,1,0:T(8,128)S(1)}, u32[]{:S(2)}, u32[]{:S(2)}) collective-permute-start(f32[1,16,256]{2,1,0:T(8,128)S(1)} %get-tuple-element.135), channel_id=1, source_target_pairs={{0,4},{4,8},{8,12},{1,5},{5,9},{9,13},{2,6},{6,10},{10,14},{3,7},{... | collective-permute-start | bytes 49160 | tf_op jit(solution)/shard_map/ppermute | solution.py:19
  435.9 7.2 collective-permute-start.38
  437.3 12.3 %collective-permute-start.44 = (f32[34,1,256]{2,1,0:T(1,128)S(1)}, f32[34,1,256]{2,1,0:T(1,128)S(1)}, u32[]{:S(2)}, u32[]{:S(2)}) collective-permute-start(f32[34,1,256]{2,1,0:T(1,128)S(1)} %get-tuple-element.79), channel_id=1, source_target_pairs={{1,0},{2,1},{3,2},{5,4},{6,5},{7,6},{9,8},{10,9},{11,10},{13,12},{... | collective-permute-start | bytes 104456 | tf_op jit(solution)/shard_map/ppermute | solution.py:21
  438.6 11.0 %collective-permute-start.45 = (f32[34,1,256]{2,1,0:T(1,128)S(1)}, f32[34,1,256]{2,1,0:T(1,128)S(1)}, u32[]{:S(2)}, u32[]{:S(2)}) collective-permute-start(f32[34,1,256]{2,1,0:T(1,128)S(1)} %get-tuple-element.80), channel_id=1, source_target_pairs={{0,1},{1,2},{2,3},{4,5},{5,6},{6,7},{8,9},{9,10},{10,11},{12,13},{... | collective-permute-start | bytes 104456 | tf_op jit(solution)/shard_map/ppermute | solution.py:19
  515.0 10.4 %collective-permute-start.50 = (f32[1,16,256]{2,1,0:T(8,128)S(1)}, f32[1,16,256]{2,1,0:T(8,128)S(1)}, u32[]{:S(2)}, u32[]{:S(2)}) collective-permute-start(f32[1,16,256]{2,1,0:T(8,128)S(1)} %get-tuple-element.124), channel_id=1, source_target_pairs={{4,0},{8,4},{12,8},{5,1},{9,5},{13,9},{6,2},{10,6},{14,10},{7,3},{... | collective-permute-start | bytes 49160 | tf_op jit(solution)/shard_map/ppermute | solution.py:21
  641.8 11.6 %collective-permute-start.64 = (f32[1,16,256]{2,1,0:T(8,128)S(1)}, f32[1,16,256]{2,1,0:T(8,128)S(1)}, u32[]{:S(2)}, u32[]{:S(2)}) collective-permute-start(f32[1,16,256]{2,1,0:T(8,128)S(1)} %get-tuple-element.117), channel_id=1, source_target_pairs={{0,4},{4,8},{8,12},{1,5},{5,9},{9,13},{2,6},{6,10},{10,14},{3,7},{... | collective-permute-start | bytes 49160 | tf_op jit(solution)/shard_map/ppermute | solution.py:19
  643.1 10.3 %collective-permute-start.63 = (f32[1,16,256]{2,1,0:T(8,128)S(1)}, f32[1,16,256]{2,1,0:T(8,128)S(1)}, u32[]{:S(2)}, u32[]{:S(2)}) collective-permute-start(f32[1,16,256]{2,1,0:T(8,128)S(1)} %get-tuple-element.118), channel_id=1, source_target_pairs={{4,0},{8,4},{12,8},{5,1},{9,5},{13,9},{6,2},{10,6},{14,10},{7,3},{... | collective-permute-start | bytes 49160 | tf_op jit(solution)/shard_map/ppermute | solution.py:21
  644.9 14.4 %collective-permute-start.60 = (f32[1,16,256]{2,1,0:T(8,128)S(1)}, f32[1,16,256]{2,1,0:T(8,128)S(1)}, u32[]{:S(2)}, u32[]{:S(2)}) collective-permute-start(f32[1,16,256]{2,1,0:T(8,128)S(1)} %get-tuple-element.115), channel_id=1, source_target_pairs={{0,4},{4,8},{8,12},{1,5},{5,9},{9,13},{2,6},{6,10},{10,14},{3,7},{... | collective-permute-start | bytes 49160 | tf_op jit(solution)/shard_map/ppermute | solution.py:19
  652.1 7.2 collective-permute-start.59
  653.4 12.2 %collective-permute-start.65 = (f32[34,1,256]{2,1,0:T(1,128)S(1)}, f32[34,1,256]{2,1,0:T(1,128)S(1)}, u32[]{:S(2)}, u32[]{:S(2)}) collective-permute-start(f32[34,1,256]{2,1,0:T(1,128)S(1)} %get-tuple-element.69), channel_id=1, source_target_pairs={{1,0},{2,1},{3,2},{5,4},{6,5},{7,6},{9,8},{10,9},{11,10},{13,12},{... | collective-permute-start | bytes 104456 | tf_op jit(solution)/shard_map/ppermute | solution.py:21
  654.7 10.9 %collective-permute-start.66 = (f32[34,1,256]{2,1,0:T(1,128)S(1)}, f32[34,1,256]{2,1,0:T(1,128)S(1)}, u32[]{:S(2)}, u32[]{:S(2)}) collective-permute-start(f32[34,1,256]{2,1,0:T(1,128)S(1)} %get-tuple-element.70), channel_id=1, source_target_pairs={{0,1},{1,2},{2,3},{4,5},{5,6},{6,7},{8,9},{9,10},{10,11},{12,13},{... | collective-permute-start | bytes 104456 | tf_op jit(solution)/shard_map/ppermute | solution.py:19
  731.3 10.4 %collective-permute-start.71 = (f32[1,16,256]{2,1,0:T(8,128)S(1)}, f32[1,16,256]{2,1,0:T(8,128)S(1)}, u32[]{:S(2)}, u32[]{:S(2)}) collective-permute-start(f32[1,16,256]{2,1,0:T(8,128)S(1)} %get-tuple-element.104), channel_id=1, source_target_pairs={{4,0},{8,4},{12,8},{5,1},{9,5},{13,9},{6,2},{10,6},{14,10},{7,3},{... | collective-permute-start | bytes 49160 | tf_op jit(solution)/shard_map/ppermute | solution.py:21
  797.7 6.9 collective-permute-start.75
  (65 other events, 358.7 us)
where the time goes:
time: 861 us; the launch traced here: 858 us
  blocking collectives  477 us (55%)
  starting transfers between devices  204 us (24%)
  waiting for transfers between devices  103 us (12%)
  between operations  39.6 us (5%)
  other arithmetic  27.4 us (3%)
    psum x12, blocking collectives, two_products(): lax.psum((jnp.sum(resid * resid), jnp.sum(resid * image)), ('gx', 'yz'))  477 us
    ppermute x38, starting transfers between devices, extended(): lax.ppermute(tail, axis, [(i, (i + 1) % count) for i in range(ends)])  150 us
    ppermute x38, waiting for transfers between devices, extended(): lax.ppermute(head, axis, [((i + 1) % count, i) for i in range(ends)])  79.6 us
    ppermute x38, starting transfers between devices, extended(): lax.ppermute(head, axis, [((i + 1) % count, i) for i in range(ends)])  49.4 us
    ppermute x38, waiting for transfers between devices, extended(): lax.ppermute(tail, axis, [(i, (i + 1) % count) for i in range(ends)])  23.4 us
  transfers between devices with their start and end apart: 79, of which 42 were waited for; matrix products, arithmetic and copies ran while one was open for 1% of the time, Pallas kernels for 0%

commit v1 on v0

--- a/solution.py
+++ b/solution.py
@@ -1,3 +1,4 @@
+import functools
 import jax
 import jax.numpy as jnp
 from jax import lax
@@ -6,6 +7,15 @@
 STEPS = 3
 ITERS = 3
 diffusion_number = 1.0
+
+
+def deliver_rows_in(local_array, lane_axis, link_axis):
+    for k0 in (lane_axis, link_axis):
+        local_array = lax.psum(local_array, axis_name=k0)
+    return local_array
+
+
+register_records = functools.partial(deliver_rows_in, lane_axis="gx", link_axis="yz")
 
 
 def extended(cells, sides, width):
@@ -46,7 +56,7 @@
 
 
 def two_products(resid, image):
-    return lax.psum((jnp.sum(resid * resid), jnp.sum(resid * image)), ("gx", "yz"))
+    return register_records((jnp.sum(resid * resid), jnp.sum(resid * image)))
 
 
 def solve(target, guess, damping):

time: 861 us -> 641 us (0.74)
  blocking collectives: 477 us -> 272 us
  waiting for transfers between devices: 103 us -> 88.5 us
    psum x12 -> x24, blocking collectives: 477 us -> 272 us  [deliver_rows_in(): local_array = lax.psum(local_array, axis_name=k0)]
    ppermute x38, waiting for transfers between devices: 79.6 us -> 64.9 us  [extended(): lax.ppermute(head, axis, [((i + 1) % count, i) for i in range(ends)])]
where the time goes in v1:
time: 641 us; the launch traced here: 637 us
  blocking collectives  272 us (42%)
  starting transfers between devices  203 us (32%)
  waiting for transfers between devices  88.5 us (14%)
  between operations  39.3 us (6%)
  other arithmetic  27.1 us (4%)
  local copies, waits for them, and re-layouts  7.39 us (1%)
    psum x24, blocking collectives, deliver_rows_in(): local_array = lax.psum(local_array, axis_name=k0)  272 us
    ppermute x38, starting transfers between devices, extended(): lax.ppermute(tail, axis, [(i, (i + 1) % count) for i in range(ends)])  150 us
    ppermute x38, waiting for transfers between devices, extended(): lax.ppermute(head, axis, [((i + 1) % count, i) for i in range(ends)])  64.9 us
    ppermute x38, starting transfers between devices, extended(): lax.ppermute(head, axis, [((i + 1) % count, i) for i in range(ends)])  49.5 us
    ppermute x38, waiting for transfers between devices, extended(): lax.ppermute(tail, axis, [(i, (i + 1) % count) for i in range(ends)])  23.6 us
    reduce_sum x12, other arithmetic, two_products(): return register_records((jnp.sum(resid * resid), jnp.sum(resid * image)))  16 us
  transfers between devices with their start and end apart: 79, of which 42 were waited for; matrix products, arithmetic and copies ran while one was open for 1% of the time, Pallas kernels for 0%

profile of v1, /device:TPU:0, one launch (start us, length us, event | category | flops | bytes accessed | tf_op | source)
XLA Modules:
  0.0 637.2 jit_solution(12951947392990534814)
XLA Ops:
  38.2 9.6 %all-reduce.61 = (f32[]{:T(128)}, f32[]{:T(128)}) all-reduce(f32[]{:T(128)} %get-tuple-element.28, f32[]{:T(128)} %get-tuple-element.27), channel_id=1, replica_groups=mesh['level'=2,'gx'=4,'yz'=4] {'gx'}, use_global_device_ids=true, to_apply=%region_1.2 | all-reduce | flops 2 | bytes 16 | tf_op jit(solution)/shard_map/psum | solution.py:14
  47.9 13.8 %all-reduce.49 = (f32[]{:T(128)}, f32[]{:T(128)}) all-reduce(f32[]{:T(128)} %get-tuple-element.75, f32[]{:T(128)} %get-tuple-element.76), channel_id=1, replica_groups=mesh['level'=2,'gx'=4,'yz'=4] {'yz'}, use_global_device_ids=true, to_apply=%region_2.3 | all-reduce | flops 2 | bytes 16 | tf_op jit(solution)/shard_map/psum | solution.py:14
  80.8 11.0 %all-reduce.60 = (f32[]{:T(128)}, f32[]{:T(128)}) all-reduce(f32[]{:T(128)} %get-tuple-element.26, f32[]{:T(128)} %get-tuple-element.25), channel_id=1, replica_groups=mesh['level'=2,'gx'=4,'yz'=4] {'gx'}, use_global_device_ids=true, to_apply=%region_7.8 | all-reduce | flops 2 | bytes 16 | tf_op jit(solution)/shard_map/psum | solution.py:14
  91.8 11.3 %all-reduce.48 = (f32[]{:T(128)}, f32[]{:T(128)}) all-reduce(f32[]{:T(128)} %get-tuple-element.73, f32[]{:T(128)} %get-tuple-element.74), channel_id=1, replica_groups=mesh['level'=2,'gx'=4,'yz'=4] {'yz'}, use_global_device_ids=true, to_apply=%region_8.9 | all-reduce | flops 2 | bytes 16 | tf_op jit(solution)/shard_map/psum | solution.py:14
  125.8 11.0 %all-reduce.59 = (f32[]{:T(128)}, f32[]{:T(128)}) all-reduce(f32[]{:T(128)} %get-tuple-element.24, f32[]{:T(128)} %get-tuple-element.23), channel_id=1, replica_groups=mesh['level'=2,'gx'=4,'yz'=4] {'gx'}, use_global_device_ids=true, to_apply=%region_13.14 | all-reduce | flops 2 | bytes 16 | tf_op jit(solution)/shard_map/psum | solution.py:14
  136.7 11.3 %all-reduce.47 = (f32[]{:T(128)}, f32[]{:T(128)}) all-reduce(f32[]{:T(128)} %get-tuple-element.71, f32[]{:T(128)} %get-tuple-element.72), channel_id=1, replica_groups=mesh['level'=2,'gx'=4,'yz'=4] {'yz'}, use_global_device_ids=true, to_apply=%region_14.15 | all-reduce | flops 2 | bytes 16 | tf_op jit(solution)/shard_map/psum | solution.py:14
  199.8 11.0 %all-reduce.58 = (f32[]{:T(128)}, f32[]{:T(128)}) all-reduce(f32[]{:T(128)} %get-tuple-element.22, f32[]{:T(128)} %get-tuple-element.21), channel_id=1, replica_groups=mesh['level'=2,'gx'=4,'yz'=4] {'gx'}, use_global_device_ids=true, to_apply=%region_19.20 | all-reduce | flops 2 | bytes 16 | tf_op jit(solution)/shard_map/psum | solution.py:14
  210.8 12.3 %all-reduce.46 = (f32[]{:T(128)}, f32[]{:T(128)}) all-reduce(f32[]{:T(128)} %get-tuple-element.69, f32[]{:T(128)} %get-tuple-element.70), channel_id=1, replica_groups=mesh['level'=2,'gx'=4,'yz'=4] {'yz'}, use_global_device_ids=true, to_apply=%region_20.21 | all-reduce | flops 2 | bytes 16 | tf_op jit(solution)/shard_map/psum | solution.py:14
  242.3 11.0 %all-reduce.57 = (f32[]{:T(128)}, f32[]{:T(128)}) all-reduce(f32[]{:T(128)} %get-tuple-element.20, f32[]{:T(128)} %get-tuple-element.19), channel_id=1, replica_groups=mesh['level'=2,'gx'=4,'yz'=4] {'gx'}, use_global_device_ids=true, to_apply=%region_25.26 | all-reduce | flops 2 | bytes 16 | tf_op jit(solution)/shard_map/psum | solution.py:14
  253.3 11.3 %all-reduce.45 = (f32[]{:T(128)}, f32[]{:T(128)}) all-reduce(f32[]{:T(128)} %get-tuple-element.67, f32[]{:T(128)} %get-tuple-element.68), channel_id=1, replica_groups=mesh['level'=2,'gx'=4,'yz'=4] {'yz'}, use_global_device_ids=true, to_apply=%region_26.27 | all-reduce | flops 2 | bytes 16 | tf_op jit(solution)/shard_map/psum | solution.py:14
  287.3 11.0 %all-reduce.56 = (f32[]{:T(128)}, f32[]{:T(128)}) all-reduce(f32[]{:T(128)} %get-tuple-element.18, f32[]{:T(128)} %get-tuple-element.17), channel_id=1, replica_groups=mesh['level'=2,'gx'=4,'yz'=4] {'gx'}, use_global_device_ids=true, to_apply=%region_31.32 | all-reduce | flops 2 | bytes 16 | tf_op jit(solution)/shard_map/psum | solution.py:14
  298.3 11.3 %all-reduce.44 = (f32[]{:T(128)}, f32[]{:T(128)}) all-reduce(f32[]{:T(128)} %get-tuple-element.65, f32[]{:T(128)} %get-tuple-element.66), channel_id=1, replica_groups=mesh['level'=2,'gx'=4,'yz'=4] {'yz'}, use_global_device_ids=true, to_apply=%region_32.33 | all-reduce | flops 2 | bytes 16 | tf_op jit(solution)/shard_map/psum | solution.py:14
  361.7 11.0 %all-reduce.55 = (f32[]{:T(128)}, f32[]{:T(128)}) all-reduce(f32[]{:T(128)} %get-tuple-element.16, f32[]{:T(128)} %get-tuple-element.15), channel_id=1, replica_groups=mesh['level'=2,'gx'=4,'yz'=4] {'gx'}, use_global_device_ids=true, to_apply=%region_37.38 | all-reduce | flops 2 | bytes 16 | tf_op jit(solution)/shard_map/psum | solution.py:14
  372.7 12.2 %all-reduce.43 = (f32[]{:T(128)}, f32[]{:T(128)}) all-reduce(f32[]{:T(128)} %get-tuple-element.63, f32[]{:T(128)} %get-tuple-element.64), channel_id=1, replica_groups=mesh['level'=2,'gx'=4,'yz'=4] {'yz'}, use_global_device_ids=true, to_apply=%region_38.39 | all-reduce | flops 2 | bytes 16 | tf_op jit(solution)/shard_map/psum | solution.py:14
  404.2 11.0 %all-reduce.54 = (f32[]{:T(128)}, f32[]{:T(128)}) all-reduce(f32[]{:T(128)} %get-tuple-element.14, f32[]{:T(128)} %get-tuple-element.13), channel_id=1, replica_groups=mesh['level'=2,'gx'=4,'yz'=4] {'gx'}, use_global_device_ids=true, to_apply=%region_43.44 | all-reduce | flops 2 | bytes 16 | tf_op jit(solution)/shard_map/psum | solution.py:14
  415.2 11.3 %all-reduce.42 = (f32[]{:T(128)}, f32[]{:T(128)}) all-reduce(f32[]{:T(128)} %get-tuple-element.61, f32[]{:T(128)} %get-tuple-element.62), channel_id=1, replica_groups=mesh['level'=2,'gx'=4,'yz'=4] {'yz'}, use_global_device_ids=true, to_apply=%region_44.45 | all-reduce | flops 2 | bytes 16 | tf_op jit(solution)/shard_map/psum | solution.py:14
  449.2 11.0 %all-reduce.53 = (f32[]{:T(128)}, f32[]{:T(128)}) all-reduce(f32[]{:T(128)} %get-tuple-element.12, f32[]{:T(128)} %get-tuple-element.11), channel_id=1, replica_groups=mesh['level'=2,'gx'=4,'yz'=4] {'gx'}, use_global_device_ids=true, to_apply=%region_49.50 | all-reduce | flops 2 | bytes 16 | tf_op jit(solution)/shard_map/psum | solution.py:14
  460.2 11.3 %all-reduce.41 = (f32[]{:T(128)}, f32[]{:T(128)}) all-reduce(f32[]{:T(128)} %get-tuple-element.59, f32[]{:T(128)} %get-tuple-element.60), channel_id=1, replica_groups=mesh['level'=2,'gx'=4,'yz'=4] {'yz'}, use_global_device_ids=true, to_apply=%region_50.51 | all-reduce | flops 2 | bytes 16 | tf_op jit(solution)/shard_map/psum | solution.py:14
  522.7 11.0 %all-reduce.52 = (f32[]{:T(128)}, f32[]{:T(128)}) all-reduce(f32[]{:T(128)} %get-tuple-element.10, f32[]{:T(128)} %get-tuple-element.9), channel_id=1, replica_groups=mesh['level'=2,'gx'=4,'yz'=4] {'gx'}, use_global_device_ids=true, to_apply=%region_55.56 | all-reduce | flops 2 | bytes 16 | tf_op jit(solution)/shard_map/psum | solution.py:14
  533.7 12.2 %all-reduce.40 = (f32[]{:T(128)}, f32[]{:T(128)}) all-reduce(f32[]{:T(128)} %get-tuple-element.57, f32[]{:T(128)} %get-tuple-element.58), channel_id=1, replica_groups=mesh['level'=2,'gx'=4,'yz'=4] {'yz'}, use_global_device_ids=true, to_apply=%region_56.57 | all-reduce | flops 2 | bytes 16 | tf_op jit(solution)/shard_map/psum | solution.py:14
  565.1 11.0 %all-reduce.51 = (f32[]{:T(128)}, f32[]{:T(128)}) all-reduce(f32[]{:T(128)} %get-tuple-element.8, f32[]{:T(128)} %get-tuple-element.7), channel_id=1, replica_groups=mesh['level'=2,'gx'=4,'yz'=4] {'gx'}, use_global_device_ids=true, to_apply=%region_61.62 | all-reduce | flops 2 | bytes 16 | tf_op jit(solution)/shard_map/psum | solution.py:14
  576.1 11.3 %all-reduce.39 = (f32[]{:T(128)}, f32[]{:T(128)}) all-reduce(f32[]{:T(128)} %get-tuple-element.55, f32[]{:T(128)} %get-tuple-element.56), channel_id=1, replica_groups=mesh['level'=2,'gx'=4,'yz'=4] {'yz'}, use_global_device_ids=true, to_apply=%region_62.63 | all-reduce | flops 2 | bytes 16 | tf_op jit(solution)/shard_map/psum | solution.py:14
  610.0 11.0 %all-reduce.50 = (f32[]{:T(128)}, f32[]{:T(128)}) all-reduce(f32[]{:T(128)} %get-tuple-element.6, f32[]{:T(128)} %get-tuple-element.5), channel_id=1, replica_groups=mesh['level'=2,'gx'=4,'yz'=4] {'gx'}, use_global_device_ids=true, to_apply=%region_67.68 | all-reduce | flops 2 | bytes 16 | tf_op jit(solution)/shard_map/psum | solution.py:14
  621.0 11.3 %all-reduce.38 = (f32[]{:T(128)}, f32[]{:T(128)}) all-reduce(f32[]{:T(128)} %get-tuple-element.53, f32[]{:T(128)} %get-tuple-element.54), channel_id=1, replica_groups=mesh['level'=2,'gx'=4,'yz'=4] {'yz'}, use_global_device_ids=true, to_apply=%region_68.69 | all-reduce | flops 2 | bytes 16 | tf_op jit(solution)/shard_map/psum | solution.py:14
  (269 shorter events, 326.1 us)
Async XLA Ops:
  153.5 11.0 %collective-permute-start.22 = (f32[1,16,256]{2,1,0:T(8,128)S(1)}, f32[1,16,256]{2,1,0:T(8,128)S(1)}, u32[]{:S(2)}, u32[]{:S(2)}) collective-permute-start(f32[1,16,256]{2,1,0:T(8,128)S(1)} %get-tuple-element.181), channel_id=1, source_target_pairs={{0,4},{4,8},{8,12},{1,5},{5,9},{9,13},{2,6},{6,10},{10,14},{3,7},{... | collective-permute-start | bytes 49160 | tf_op jit(solution)/shard_map/ppermute | solution.py:29
  155.1 9.3 %collective-permute-start.21 = (f32[1,16,256]{2,1,0:T(8,128)S(1)}, f32[1,16,256]{2,1,0:T(8,128)S(1)}, u32[]{:S(2)}, u32[]{:S(2)}) collective-permute-start(f32[1,16,256]{2,1,0:T(8,128)S(1)} %get-tuple-element.182), channel_id=1, source_target_pairs={{4,0},{8,4},{12,8},{5,1},{9,5},{13,9},{6,2},{10,6},{14,10},{7,3},{... | collective-permute-start | bytes 49160 | tf_op jit(solution)/shard_map/ppermute | solution.py:31
  157.5 12.9 %collective-permute-start.18 = (f32[1,16,256]{2,1,0:T(8,128)S(1)}, f32[1,16,256]{2,1,0:T(8,128)S(1)}, u32[]{:S(2)}, u32[]{:S(2)}) collective-permute-start(f32[1,16,256]{2,1,0:T(8,128)S(1)} %get-tuple-element.179), channel_id=1, source_target_pairs={{0,4},{4,8},{8,12},{1,5},{5,9},{9,13},{2,6},{6,10},{10,14},{3,7},{... | collective-permute-start | bytes 49160 | tf_op jit(solution)/shard_map/ppermute | solution.py:29
  163.2 7.2 %collective-permute-start.17 = (f32[1,16,256]{2,1,0:T(8,128)S(1)}, f32[1,16,256]{2,1,0:T(8,128)S(1)}, u32[]{:S(2)}, u32[]{:S(2)}) collective-permute-start(f32[1,16,256]{2,1,0:T(8,128)S(1)} %get-tuple-element.180), channel_id=1, source_target_pairs={{4,0},{8,4},{12,8},{5,1},{9,5},{13,9},{6,2},{10,6},{14,10},{7,3},{... | collective-permute-start | bytes 49160 | tf_op jit(solution)/shard_map/ppermute | solution.py:31
  164.6 12.2 %collective-permute-start.23 = (f32[34,1,256]{2,1,0:T(1,128)S(1)}, f32[34,1,256]{2,1,0:T(1,128)S(1)}, u32[]{:S(2)}, u32[]{:S(2)}) collective-permute-start(f32[34,1,256]{2,1,0:T(1,128)S(1)} %get-tuple-element.113), channel_id=1, source_target_pairs={{1,0},{2,1},{3,2},{5,4},{6,5},{7,6},{9,8},{10,9},{11,10},{13,12},{... | collective-permute-start | bytes 104456 | tf_op jit(solution)/shard_map/ppermute | solution.py:31
  165.9 10.9 %collective-permute-start.24 = (f32[34,1,256]{2,1,0:T(1,128)S(1)}, f32[34,1,256]{2,1,0:T(1,128)S(1)}, u32[]{:S(2)}, u32[]{:S(2)}) collective-permute-start(f32[34,1,256]{2,1,0:T(1,128)S(1)} %get-tuple-element.114), channel_id=1, source_target_pairs={{0,1},{1,2},{2,3},{4,5},{5,6},{6,7},{8,9},{9,10},{10,11},{12,13},{... | collective-permute-start | bytes 104456 | tf_op jit(solution)/shard_map/ppermute | solution.py:29
  178.9 6.9 %collective-permute-start.26 = (f32[1,16,256]{2,1,0:T(8,128)S(1)}, f32[1,16,256]{2,1,0:T(8,128)S(1)}, u32[]{:S(2)}, u32[]{:S(2)}) collective-permute-start(f32[1,16,256]{2,1,0:T(8,128)S(1)} %get-tuple-element.171), channel_id=1, source_target_pairs={{0,4},{4,8},{8,12},{1,5},{5,9},{9,13},{2,6},{6,10},{10,14},{3,7},{... | collective-permute-start | bytes 49160 | tf_op jit(solution)/shard_map/ppermute | solution.py:29
  226.1 6.8 %collective-permute-start.29 = (f32[1,16,256]{2,1,0:T(8,128)S(1)}, f32[1,16,256]{2,1,0:T(8,128)S(1)}, u32[]{:S(2)}, u32[]{:S(2)}) collective-permute-start(f32[1,16,256]{2,1,0:T(8,128)S(1)} %get-tuple-element.168), channel_id=1, source_target_pairs={{4,0},{8,4},{12,8},{5,1},{9,5},{13,9},{6,2},{10,6},{14,10},{7,3},{... | collective-permute-start | bytes 49160 | tf_op jit(solution)/shard_map/ppermute | solution.py:31
  315.1 11.3 %collective-permute-start.43 = (f32[1,16,256]{2,1,0:T(8,128)S(1)}, f32[1,16,256]{2,1,0:T(8,128)S(1)}, u32[]{:S(2)}, u32[]{:S(2)}) collective-permute-start(f32[1,16,256]{2,1,0:T(8,128)S(1)} %get-tuple-element.161), channel_id=1, source_target_pairs={{0,4},{4,8},{8,12},{1,5},{5,9},{9,13},{2,6},{6,10},{10,14},{3,7},{... | collective-permute-start | bytes 49160 | tf_op jit(solution)/shard_map/ppermute | solution.py:29
  316.7 9.7 %collective-permute-start.42 = (f32[1,16,256]{2,1,0:T(8,128)S(1)}, f32[1,16,256]{2,1,0:T(8,128)S(1)}, u32[]{:S(2)}, u32[]{:S(2)}) collective-permute-start(f32[1,16,256]{2,1,0:T(8,128)S(1)} %get-tuple-element.162), channel_id=1, source_target_pairs={{4,0},{8,4},{12,8},{5,1},{9,5},{13,9},{6,2},{10,6},{14,10},{7,3},{... | collective-permute-start | bytes 49160 | tf_op jit(solution)/shard_map/ppermute | solution.py:31
  319.2 13.1 %collective-permute-start.39 = (f32[1,16,256]{2,1,0:T(8,128)S(1)}, f32[1,16,256]{2,1,0:T(8,128)S(1)}, u32[]{:S(2)}, u32[]{:S(2)}) collective-permute-start(f32[1,16,256]{2,1,0:T(8,128)S(1)} %get-tuple-element.159), channel_id=1, source_target_pairs={{0,4},{4,8},{8,12},{1,5},{5,9},{9,13},{2,6},{6,10},{10,14},{3,7},{... | collective-permute-start | bytes 49160 | tf_op jit(solution)/shard_map/ppermute | solution.py:29
  324.9 7.4 %collective-permute-start.38 = (f32[1,16,256]{2,1,0:T(8,128)S(1)}, f32[1,16,256]{2,1,0:T(8,128)S(1)}, u32[]{:S(2)}, u32[]{:S(2)}) collective-permute-start(f32[1,16,256]{2,1,0:T(8,128)S(1)} %get-tuple-element.160), channel_id=1, source_target_pairs={{4,0},{8,4},{12,8},{5,1},{9,5},{13,9},{6,2},{10,6},{14,10},{7,3},{... | collective-permute-start | bytes 49160 | tf_op jit(solution)/shard_map/ppermute | solution.py:31
  326.5 12.2 %collective-permute-start.44 = (f32[34,1,256]{2,1,0:T(1,128)S(1)}, f32[34,1,256]{2,1,0:T(1,128)S(1)}, u32[]{:S(2)}, u32[]{:S(2)}) collective-permute-start(f32[34,1,256]{2,1,0:T(1,128)S(1)} %get-tuple-element.103), channel_id=1, source_target_pairs={{1,0},{2,1},{3,2},{5,4},{6,5},{7,6},{9,8},{10,9},{11,10},{13,12},{... | collective-permute-start | bytes 104456 | tf_op jit(solution)/shard_map/ppermute | solution.py:31
  327.8 10.9 %collective-permute-start.45 = (f32[34,1,256]{2,1,0:T(1,128)S(1)}, f32[34,1,256]{2,1,0:T(1,128)S(1)}, u32[]{:S(2)}, u32[]{:S(2)}) collective-permute-start(f32[34,1,256]{2,1,0:T(1,128)S(1)} %get-tuple-element.104), channel_id=1, source_target_pairs={{0,1},{1,2},{2,3},{4,5},{5,6},{6,7},{8,9},{9,10},{10,11},{12,13},{... | collective-permute-start | bytes 104456 | tf_op jit(solution)/shard_map/ppermute | solution.py:29
  340.8 6.9 %collective-permute-start.47 = (f32[1,16,256]{2,1,0:T(8,128)S(1)}, f32[1,16,256]{2,1,0:T(8,128)S(1)}, u32[]{:S(2)}, u32[]{:S(2)}) collective-permute-start(f32[1,16,256]{2,1,0:T(8,128)S(1)} %get-tuple-element.151), channel_id=1, source_target_pairs={{0,4},{4,8},{8,12},{1,5},{5,9},{9,13},{2,6},{6,10},{10,14},{3,7},{... | collective-permute-start | bytes 49160 | tf_op jit(solution)/shard_map/ppermute | solution.py:29
  388.0 6.8 %collective-permute-start.50 = (f32[1,16,256]{2,1,0:T(8,128)S(1)}, f32[1,16,256]{2,1,0:T(8,128)S(1)}, u32[]{:S(2)}, u32[]{:S(2)}) collective-permute-start(f32[1,16,256]{2,1,0:T(8,128)S(1)} %get-tuple-element.148), channel_id=1, source_target_pairs={{4,0},{8,4},{12,8},{5,1},{9,5},{13,9},{6,2},{10,6},{14,10},{7,3},{... | collective-permute-start | bytes 49160 | tf_op jit(solution)/shard_map/ppermute | solution.py:31
  433.8 6.8 %collective-permute-start.54 = (f32[1,16,256]{2,1,0:T(8,128)S(1)}, f32[1,16,256]{2,1,0:T(8,128)S(1)}, u32[]{:S(2)}, u32[]{:S(2)}) collective-permute-start(f32[1,16,256]{2,1,0:T(8,128)S(1)} %get-tuple-element.146), channel_id=1, source_target_pairs={{4,0},{8,4},{12,8},{5,1},{9,5},{13,9},{6,2},{10,6},{14,10},{7,3},{... | collective-permute-start | bytes 49160 | tf_op jit(solution)/shard_map/ppermute | solution.py:31
  477.0 10.5 %collective-permute-start.64 = (f32[1,16,256]{2,1,0:T(8,128)S(1)}, f32[1,16,256]{2,1,0:T(8,128)S(1)}, u32[]{:S(2)}, u32[]{:S(2)}) collective-permute-start(f32[1,16,256]{2,1,0:T(8,128)S(1)} %get-tuple-element.141), channel_id=1, source_target_pairs={{0,4},{4,8},{8,12},{1,5},{5,9},{9,13},{2,6},{6,10},{10,14},{3,7},{... | collective-permute-start | bytes 49160 | tf_op jit(solution)/shard_map/ppermute | solution.py:29
  478.6 8.8 %collective-permute-start.63 = (f32[1,16,256]{2,1,0:T(8,128)S(1)}, f32[1,16,256]{2,1,0:T(8,128)S(1)}, u32[]{:S(2)}, u32[]{:S(2)}) collective-permute-start(f32[1,16,256]{2,1,0:T(8,128)S(1)} %get-tuple-element.142), channel_id=1, source_target_pairs={{4,0},{8,4},{12,8},{5,1},{9,5},{13,9},{6,2},{10,6},{14,10},{7,3},{... | collective-permute-start | bytes 49160 | tf_op jit(solution)/shard_map/ppermute | solution.py:31
  480.4 13.0 %collective-permute-start.60 = (f32[1,16,256]{2,1,0:T(8,128)S(1)}, f32[1,16,256]{2,1,0:T(8,128)S(1)}, u32[]{:S(2)}, u32[]{:S(2)}) collective-permute-start(f32[1,16,256]{2,1,0:T(8,128)S(1)} %get-tuple-element.139), channel_id=1, source_target_pairs={{0,4},{4,8},{8,12},{1,5},{5,9},{9,13},{2,6},{6,10},{10,14},{3,7},{... | collective-permute-start | bytes 49160 | tf_op jit(solution)/shard_map/ppermute | solution.py:29
  486.1 7.2 %collective-permute-start.59 = (f32[1,16,256]{2,1,0:T(8,128)S(1)}, f32[1,16,256]{2,1,0:T(8,128)S(1)}, u32[]{:S(2)}, u32[]{:S(2)}) collective-permute-start(f32[1,16,256]{2,1,0:T(8,128)S(1)} %get-tuple-element.140), channel_id=1, source_target_pairs={{4,0},{8,4},{12,8},{5,1},{9,5},{13,9},{6,2},{10,6},{14,10},{7,3},{... | collective-permute-start | bytes 49160 | tf_op jit(solution)/shard_map/ppermute | solution.py:31
  487.5 12.2 %collective-permute-start.65 = (f32[34,1,256]{2,1,0:T(1,128)S(1)}, f32[34,1,256]{2,1,0:T(1,128)S(1)}, u32[]{:S(2)}, u32[]{:S(2)}) collective-permute-start(f32[34,1,256]{2,1,0:T(1,128)S(1)} %get-tuple-element.93), channel_id=1, source_target_pairs={{1,0},{2,1},{3,2},{5,4},{6,5},{7,6},{9,8},{10,9},{11,10},{13,12},{... | collective-permute-start | bytes 104456 | tf_op jit(solution)/shard_map/ppermute | solution.py:31
  488.8 10.9 %collective-permute-start.66 = (f32[34,1,256]{2,1,0:T(1,128)S(1)}, f32[34,1,256]{2,1,0:T(1,128)S(1)}, u32[]{:S(2)}, u32[]{:S(2)}) collective-permute-start(f32[34,1,256]{2,1,0:T(1,128)S(1)} %get-tuple-element.94), channel_id=1, source_target_pairs={{0,1},{1,2},{2,3},{4,5},{5,6},{6,7},{8,9},{9,10},{10,11},{12,13},{... | collective-permute-start | bytes 104456 | tf_op jit(solution)/shard_map/ppermute | solution.py:29
  501.8 6.9 %collective-permute-start.68 = (f32[1,16,256]{2,1,0:T(8,128)S(1)}, f32[1,16,256]{2,1,0:T(8,128)S(1)}, u32[]{:S(2)}, u32[]{:S(2)}) collective-permute-start(f32[1,16,256]{2,1,0:T(8,128)S(1)} %get-tuple-element.131), channel_id=1, source_target_pairs={{0,4},{4,8},{8,12},{1,5},{5,9},{9,13},{2,6},{6,10},{10,14},{3,7},{... | collective-permute-start | bytes 49160 | tf_op jit(solution)/shard_map/ppermute | solution.py:29
  (65 other events, 361.2 us)
